TPU v7x, 32 devices: a whole 2x2x4 slice. The times are simulated.
32 devices in a mesh: expert: 4 (over y, core), shard: 8 (over z, x).
Axes of the slice: x: 2, y: 2, z: 4, core: 2. Of those that a mesh axis runs over, the one named last changes fastest.
Arguments:
- train_down: float32 [16, 6400, 4096], P('expert', None, 'shard'), may hold values from -0.109375 to 0.109375
- other_down: bfloat16 [16, 6400, 4096], P('expert', None, 'shard'), may hold values from -0.0390625 to 0.0390625
- router_weight: float32 [4096, 16], P('shard', 'expert'), may hold values from -0.09375 to 0.09375
- router_gain: float32 [4096], P('shard'), may hold values from 0.25 to 1.75
Outputs:
- ready_down: bfloat16 [16, 6400, 4096], P('expert', 'shard')
- scale_down: float32 [16, 6400], P('expert', 'shard')
- serve_router: bfloat16 [4096, 16], replicated
All inputs are finite; a program needn't handle non-finite values.
Results may differ from a plain program's by a relative error of at most 0.001.
Values may be sent and summed in bfloat16 or wider, within the bound.
A program may use at most 256 MiB of HBM per device.

v0:
```python
import jax
import jax.numpy as jnp
from jax import lax
from jax.sharding import PartitionSpec as P


def per_device(train_down, other_down, router_weight, router_gain):
    latest_down = train_down + other_down.astype(jnp.float32)
    total_down = lax.psum(jnp.sum(latest_down * latest_down, axis=2), "shard")
    scale_down = jnp.sqrt(total_down)
    narrow_down = (latest_down / jnp.expand_dims(scale_down, 2)).astype(jnp.bfloat16)
    ready_down = lax.all_to_all(narrow_down, "shard", split_axis=1, concat_axis=2, tiled=True)
    scale_down = lax.dynamic_slice_in_dim(
        scale_down, lax.axis_index("shard") * ready_down.shape[1], ready_down.shape[1], axis=1
    )
    part_router = (router_weight * router_gain[:, None]).astype(jnp.bfloat16)
    row_router = lax.all_gather(part_router, "shard", axis=0, tiled=True)
    serve_router = lax.all_gather(row_router, "expert", axis=1, tiled=True)
    return (ready_down, scale_down, serve_router)


def solution(mesh):
    in_specs = (
        P("expert", None, "shard"),
        P("expert", None, "shard"),
        P("shard", "expert"),
        P("shard"),
    )
    out_specs = (P("expert", "shard", None), P("expert", "shard"), P())
    return jax.shard_map(
        per_device, mesh=mesh, in_specs=in_specs, out_specs=out_specs, check_vma=False
    )
```

profile of v0, /device:TPU:0, one launch (start us, length us, event | category | flops | bytes accessed | tf_op | source)
XLA Modules:
  0.0 905.5 jit_solution(8188198296431997854)
XLA Ops:
  7.2 0.0 all-reduce.2.cloned.1.call-start
  7.2 24.2 %multiply_reduce_fusion = f32[4,6400]{1,0:T(4,128)S(1)} fusion(f32[4,6400,512]{2,1,0:T(8,128)} %param.4, bf16[4,6400,512]{2,1,0:T(8,128)(2,1)} %param.5), kind=kLoop, calls=%fused_computation.1 | loop fusion | flops 52403200 | bytes 78745600 | tf_op jit(solution)/shard_map/reduce_sum | solution.py:9
  31.4 2.3 copy.21
  33.7 0.0 all-reduce.2.cloned.1.call-update
  33.7 135.6 %all-reduce.2.cloned.1.call-done = f32[4,6400]{0,1:T(8,128)} async-done(((f32[4,6400]{0,1:T(8,128)}), f32[4,6400]{0,1:T(8,128)}) %all-reduce.2.cloned.1.call-update) | async-done | bytes 102416 | tf_op jit(solution)/shard_map/psum | solution.py:9
  169.3 2.7 sqrt.3
  172.0 1.2 copy.17
  173.3 34.3 %divide_convert_fusion = bf16[4,6400,512]{2,1,0:T(8,128)(2,1)} fusion(f32[4,6400,512]{2,1,0:T(8,128)} %param.4, bf16[4,6400,512]{2,1,0:T(8,128)(2,1)} %param.5, f32[4,6400]{1,0:T(4,128)S(1)} %copy.17), kind=kLoop, calls=%fused_computation | loop fusion | flops 52428800 | bytes 104960000 | tf_op jit(solution)/shard_map/convert_element_type | solution.py:11
  207.5 33.4 %copy.18 = bf16[4,6400,512]{2,0,1:T(4,128)(2,1)} copy(bf16[4,6400,512]{2,1,0:T(8,128)(2,1)} %divide_convert_fusion) | data formatting | bytes 52428800 | tf_op jit(solution)/shard_map/convert_element_type | solution.py:11
  240.9 0.0 copy-start
  240.9 0.0 copy-start.1
  240.9 6.6 all-to-all-start
  247.6 0.0 copy-done
  247.6 0.0 copy-done.1
  247.6 585.0 %all_gather.6 = bf16[4096,4]{0,1:T(4,128)(2,1)S(1)} all-gather(bf16[512,4]{0,1:T(4,128)(2,1)S(1)} %multiply_convert_fusion), channel_id=1, replica_groups=mesh['expert'=4,'shard'=8] {'shard'}, dimensions={0}, use_global_device_ids=true | all-gather | bytes 36864 | tf_op jit(solution)/shard_map/all_gather | solution.py:17
  832.7 5.4 all-gather
  838.1 0.7 reshape.9
  838.8 0.8 constant_dynamic-slice_fusion
  839.5 1.8 copy.20
  841.3 0.0 all-to-all-done
  841.3 18.2 %copy.19 = bf16[4,800,8,512]{3,2,1,0:T(8,128)(2,1)} copy(bf16[4,800,8,512]{3,0,1,2:T(4,128)(2,1)} %bitcast.1) | data formatting | bytes 52428800 | tf_op jit(solution)/shard_map/all_to_all | solution.py:12
  859.5 39.2 %all_to_all.16 = bf16[4,800,4096]{2,1,0:T(8,128)(2,1)} reshape(bf16[4,800,8,512]{3,2,1,0:T(8,128)(2,1)} %copy.19) | data formatting | bytes 52428800 | tf_op jit(solution)/shard_map/all_to_all | solution.py:12
  (1 shorter events, 0.0 us)
Async XLA Ops:
  7.2 162.2 %all-reduce.2.cloned.1.call-start = ((), (), s32[]{:S(2)}) async-start(), calls=%async_computation.1 | async-start | bytes 6553600 | tf_op jit(solution)/shard_map/psum | solution.py:9
  240.9 6.7 copy-start
  240.9 6.7 copy-start.1
  240.9 600.4 %all-to-all-start = ((bf16[4,6400,512]{2,0,1:T(4,128)(2,1)}), bf16[4,6400,512]{2,0,1:T(4,128)(2,1)}, u32[]{:S(2)}, u32[]{:S(2)}) async-start(bf16[4,6400,512]{2,0,1:T(4,128)(2,1)} %copy.18), calls=%async_computation | async-start | bytes 52428800 | tf_op jit(solution)/shard_map/all_to_all | solution.py:12
Sparse Core Ops, SparseCore 0:
  33.9 135.4 all-reduce.1
where the time goes:
time: 907 us; the launch traced here: 906 us
  blocking collectives  590 us (65%)
  waiting for transfers between devices  136 us (15%)
  local copies, waits for them, and re-layouts  100 us (11%)
  other arithmetic  58.5 us (6%)
  between operations  14.1 us (2%)
    all_gather x1, blocking collectives, per_device(): row_router = lax.all_gather(part_router, 'shard', axis=0, tiled=True)  585 us
    psum x1, waiting for transfers between devices, per_device(): total_down = lax.psum(jnp.sum(latest_down * latest_down, axis=2), 'shard')  136 us
    all_to_all x2, local copies, waits for them, and re-layouts, per_device(): lax.all_to_all(narrow_down, 'shard', split_axis=1, concat_axis=2, tiled=T...  57.4 us
    convert_element_type x1, other arithmetic, per_device(): (latest_down / jnp.expand_dims(scale_down, 2)).astype(jnp.bfloat16)  34.3 us
    convert_element_type x1, local copies, waits for them, and re-layouts, per_device(): (latest_down / jnp.expand_dims(scale_down, 2)).astype(jnp.bfloat16)  33.4 us
    reduce_sum x1, other arithmetic, per_device(): total_down = lax.psum(jnp.sum(latest_down * latest_down, axis=2), 'shard')  24.2 us
  transfers between devices with their start and end apart: 2, of which 1 were waited for; matrix products, arithmetic and copies ran while one was open for 0% of the time, Pallas kernels for 0%

commit v1 on v0

--- a/solution.py
+++ b/solution.py
@@ -5,6 +5,21 @@
 
 
 def per_device(train_down, other_down, router_weight, router_gain):
+
+    def process_marks(content, mesh_dim):
+        axis_n = lax.axis_size(mesh_dim)
+        tray = []
+        for s in [*range(1, axis_n)]:
+            tray.append((s - 1, s))
+        spare = tray + [(axis_n - 1, 0)]
+        back = content
+        sheets = [back]
+        for _ in tuple(range(axis_n - 1)):
+            back = lax.ppermute(back, mesh_dim, spare)
+            sheets += [back]
+        plain = jnp.concatenate([*reversed(sheets)], 0)
+        return jnp.roll(plain, (lax.axis_index(mesh_dim) + 1) * back.shape[0], 0)
+
     latest_down = train_down + other_down.astype(jnp.float32)
     total_down = lax.psum(jnp.sum(latest_down * latest_down, axis=2), "shard")
     scale_down = jnp.sqrt(total_down)
@@ -14,7 +29,7 @@
         scale_down, lax.axis_index("shard") * ready_down.shape[1], ready_down.shape[1], axis=1
     )
     part_router = (router_weight * router_gain[:, None]).astype(jnp.bfloat16)
-    row_router = lax.all_gather(part_router, "shard", axis=0, tiled=True)
+    row_router = process_marks(part_router, mesh_dim="shard")
     serve_router = lax.all_gather(row_router, "expert", axis=1, tiled=True)
     return (ready_down, scale_down, serve_router)
 

time: 907 us -> 912 us (level)
  blocking collectives: 590 us -> 5.42 us
  waiting for transfers between devices: 136 us -> 589 us
  starting transfers between devices: 6.67 us -> 143 us
    all_gather x1 -> x0, blocking collectives: 585 us -> none  [per_device(): row_router = lax.all_gather(part_router, 'shard', axis=0, tiled=True)]
    ppermute x0 -> x7, waiting for transfers between devices: none -> 453 us  [process_marks(): back = lax.ppermute(back, mesh_dim, spare)]
    ppermute x0 -> x7, starting transfers between devices: none -> 136 us  [process_marks(): back = lax.ppermute(back, mesh_dim, spare)]
  transfers between devices with their start and end apart: 2 -> 9, of which waited for: 1 -> 8; matrix products, arithmetic and copies ran while one was open for 0% -> 0% of each run, Pallas kernels for 0% -> 0%
where the time goes in v1:
time: 912 us; the launch traced here: 911 us
  waiting for transfers between devices  589 us (65%)
  starting transfers between devices  143 us (16%)
  local copies, waits for them, and re-layouts  100 us (11%)
  other arithmetic  58.6 us (6%)
  between operations  14.1 us (2%)
    ppermute x7, waiting for transfers between devices, process_marks(): back = lax.ppermute(back, mesh_dim, spare)  453 us
    ppermute x7, starting transfers between devices, process_marks(): back = lax.ppermute(back, mesh_dim, spare)  136 us
    psum x1, waiting for transfers between devices, per_device(): total_down = lax.psum(jnp.sum(latest_down * latest_down, axis=2), 'shard')  136 us
    all_to_all x2, local copies, waits for them, and re-layouts, per_device(): lax.all_to_all(narrow_down, 'shard', split_axis=1, concat_axis=2, tiled=T...  57.4 us
    convert_element_type x1, other arithmetic, per_device(): (latest_down / jnp.expand_dims(scale_down, 2)).astype(jnp.bfloat16)  34.3 us
    convert_element_type x1, local copies, waits for them, and re-layouts, per_device(): (latest_down / jnp.expand_dims(scale_down, 2)).astype(jnp.bfloat16)  33.4 us
    reduce_sum x1, other arithmetic, per_device(): total_down = lax.psum(jnp.sum(latest_down * latest_down, axis=2), 'shard')  24.2 us
  transfers between devices with their start and end apart: 9, of which 8 were waited for; matrix products, arithmetic and copies ran while one was open for 0% of the time, Pallas kernels for 0%

profile of v1, /device:TPU:0, one launch (start us, length us, event | category | flops | bytes accessed | tf_op | source)
XLA Modules:
  0.0 910.6 jit_solution(641777327803930614)
XLA Ops:
  7.2 24.2 %multiply_reduce_fusion = f32[4,6400]{1,0:T(4,128)S(1)} fusion(f32[4,6400,512]{2,1,0:T(8,128)} %param.4, bf16[4,6400,512]{2,1,0:T(8,128)(2,1)} %param.5), kind=kLoop, calls=%fused_computation.1 | loop fusion | flops 52403200 | bytes 78745600 | tf_op jit(solution)/shard_map/reduce_sum | solution.py:24
  31.4 2.3 copy.21
  33.7 135.6 %all-reduce.2.cloned.1.call-done = f32[4,6400]{0,1:T(8,128)} async-done(((f32[4,6400]{0,1:T(8,128)}), f32[4,6400]{0,1:T(8,128)}) %all-reduce.2.cloned.1.call-update) | async-done | bytes 102416 | tf_op jit(solution)/shard_map/psum | solution.py:24
  169.3 2.7 sqrt.3
  172.0 1.2 copy.17
  173.3 34.3 %divide_convert_fusion = bf16[4,6400,512]{2,1,0:T(8,128)(2,1)} fusion(f32[4,6400,512]{2,1,0:T(8,128)} %param.4, bf16[4,6400,512]{2,1,0:T(8,128)(2,1)} %param.5, f32[4,6400]{1,0:T(4,128)S(1)} %copy.17), kind=kLoop, calls=%fused_computation | loop fusion | flops 52428800 | bytes 104960000 | tf_op jit(solution)/shard_map/convert_element_type | solution.py:26
  207.5 33.4 %copy.18 = bf16[4,6400,512]{2,0,1:T(4,128)(2,1)} copy(bf16[4,6400,512]{2,1,0:T(8,128)(2,1)} %divide_convert_fusion) | data formatting | bytes 52428800 | tf_op jit(solution)/shard_map/convert_element_type | solution.py:26
  241.0 6.7 all-to-all-start
  247.7 1.9 collective-permute-start
  249.6 424.6 %collective-permute-done = bf16[512,4]{0,1:T(4,128)(2,1)S(1)} collective-permute-done((bf16[512,4]{0,1:T(4,128)(2,1)S(1)}, bf16[512,4]{0,1:T(4,128)(2,1)S(1)}, u32[]{:S(2)}, u32[]{:S(2)}) %collective-permute-start) | collective-permute-done | bytes 4128 | tf_op jit(solution)/shard_map/ppermute | solution.py:18
  674.2 6.4 collective-permute-done.1
  680.6 6.4 collective-permute-done.2
  687.0 129.9 %collective-permute-start.3 = (bf16[512,4]{0,1:T(4,128)(2,1)S(1)}, bf16[512,4]{0,1:T(4,128)(2,1)S(1)}, u32[]{:S(2)}, u32[]{:S(2)}) collective-permute-start(bf16[512,4]{0,1:T(4,128)(2,1)S(1)} %collective-permute-done.2), channel_id=1, source_target_pairs={{0,1},{1,2},{2,3},{3,4},{4,5},{5,6},{6,7},{7,0},{8,9},{9,10},{10,1... | collective-permute-start | bytes 12296 | tf_op jit(solution)/shard_map/ppermute | solution.py:18
  817.0 1.3 collective-permute-done.3
  818.3 3.3 collective-permute-start.4
  821.6 3.2 collective-permute-done.4
  824.9 1.3 collective-permute-start.5
  826.1 5.0 collective-permute-done.5
  831.2 6.3 collective-permute-done.6
  837.7 5.4 all-gather
  843.8 0.8 constant_dynamic-slice_fusion
  844.6 1.8 copy.20
  846.4 18.2 %copy.19 = bf16[4,800,8,512]{3,2,1,0:T(8,128)(2,1)} copy(bf16[4,800,8,512]{3,0,1,2:T(4,128)(2,1)} %bitcast.1) | data formatting | bytes 52428800 | tf_op jit(solution)/shard_map/all_to_all | solution.py:27
  864.6 39.2 %all_to_all.16 = bf16[4,800,4096]{2,1,0:T(8,128)(2,1)} reshape(bf16[4,800,8,512]{3,2,1,0:T(8,128)(2,1)} %copy.19) | data formatting | bytes 52428800 | tf_op jit(solution)/shard_map/all_to_all | solution.py:27
  (29 shorter events, 1.0 us)
Async XLA Ops:
  7.2 162.2 %all-reduce.2.cloned.1.call-start = ((), (), s32[]{:S(2)}) async-start(), calls=%async_computation.1 | async-start | bytes 6553600 | tf_op jit(solution)/shard_map/psum | solution.py:24
  241.0 6.7 copy-start
  241.0 6.7 copy-start.1
  241.0 605.4 %all-to-all-start = ((bf16[4,6400,512]{2,0,1:T(4,128)(2,1)}), bf16[4,6400,512]{2,0,1:T(4,128)(2,1)}, u32[]{:S(2)}, u32[]{:S(2)}) async-start(bf16[4,6400,512]{2,0,1:T(4,128)(2,1)} %copy.18), calls=%async_computation | async-start | bytes 52428800 | tf_op jit(solution)/shard_map/all_to_all | solution.py:27
  247.7 426.6 %collective-permute-start = (bf16[512,4]{0,1:T(4,128)(2,1)S(1)}, bf16[512,4]{0,1:T(4,128)(2,1)S(1)}, u32[]{:S(2)}, u32[]{:S(2)}) collective-permute-start(bf16[512,4]{0,1:T(4,128)(2,1)S(1)} %multiply_convert_fusion), channel_id=1, source_target_pairs={{0,1},{1,2},{2,3},{3,4},{4,5},{5,6},{6,7},{7,0},{8,9},{9,10},{10,1... | collective-permute-start | bytes 12296 | tf_op jit(solution)/shard_map/ppermute | solution.py:18
  674.2 6.4 collective-permute-start.1
  680.6 6.4 collective-permute-start.2
  687.0 131.3 %collective-permute-start.3 = (bf16[512,4]{0,1:T(4,128)(2,1)S(1)}, bf16[512,4]{0,1:T(4,128)(2,1)S(1)}, u32[]{:S(2)}, u32[]{:S(2)}) collective-permute-start(bf16[512,4]{0,1:T(4,128)(2,1)S(1)} %collective-permute-done.2), channel_id=1, source_target_pairs={{0,1},{1,2},{2,3},{3,4},{4,5},{5,6},{6,7},{7,0},{8,9},{9,10},{10,1... | collective-permute-start | bytes 12296 | tf_op jit(solution)/shard_map/ppermute | solution.py:18
  818.3 6.6 collective-permute-start.4
  824.9 6.3 collective-permute-start.5
  831.2 6.3 collective-permute-start.6
Sparse Core Ops, SparseCore 0:
  33.9 135.4 all-reduce.1
